TPU v7x, 32 devices: a 4x4x1 block of a 4x4x8 slice. The times are simulated.
32 devices in a mesh: rep: 1 (over z), vocab: 32 (over y, x, core).
Axes of the slice: x: 4, y: 4, z: 1, core: 2. Of those that a mesh axis runs over, the one named last changes fastest.
The devices are a block of a 4x4x8 slice.
Arguments:
- hidden: bfloat16 [16384, 4096], P(('rep', 'vocab'))
- w_head: bfloat16 [32768, 4096], P('vocab')
- allowed_ids: int32 [2048], P('rep')
- allowed_valid: int32 [2048], P('rep')
- target_pos: int32 [16384], P(('rep', 'vocab'))
Outputs:
- output 1: float32 [16384, 2048], P(('rep', 'vocab'))
- output 2: float32 [16384], P(('rep', 'vocab'))
All inputs are finite; a program needn't handle non-finite values.
Results may differ from a plain program's by a relative error of at most 0.001.
Values are sent between devices in bfloat16 or wider.
A program may use at most 768 MiB of HBM per device.

v0:
```python
import jax
import jax.numpy as jnp
from jax import lax
from jax.sharding import PartitionSpec as P

INV_TEMP = 1.25


def owner_layout(allowed_ids, vocab_local, shards, slot_cap, my_index):
    owner_id = allowed_ids // vocab_local
    sort_order = jnp.argsort(owner_id, stable=True)
    counts = jnp.bincount(owner_id, length=shards)
    starts = jnp.cumsum(counts) - counts
    slot_rank = jnp.argsort(sort_order) - starts[owner_id]
    padded = jnp.concatenate([sort_order, jnp.zeros((slot_cap,), sort_order.dtype)])
    mine_pos = lax.dynamic_slice(padded, (starts[my_index],), (slot_cap,))
    local_idx = jnp.clip(allowed_ids[mine_pos] - my_index * vocab_local, 0, vocab_local - 1)
    return owner_id, slot_rank, local_idx


def finish_rows(own_scores, owner_id, slot_rank, allowed_valid, target_pos, shards):
    rows_dev = target_pos.shape[0]
    outgoing = own_scores.reshape(shards, rows_dev, own_scores.shape[1])
    incoming = lax.all_to_all(outgoing, 'vocab', 0, 0)
    scores = incoming[owner_id, :, slot_rank].T
    keep_mask = (allowed_valid > 0)[None, :]
    masked = jnp.where(keep_mask, scores, -jnp.inf)
    log_norm = jax.nn.logsumexp(masked, axis=1)
    token_probs = jnp.where(keep_mask, jnp.exp(masked - log_norm[:, None]), 0.0)
    picked = jnp.take_along_axis(scores, target_pos[:, None], axis=1)[:, 0]
    return token_probs, picked - log_norm


def solution(mesh):
    shards = mesh.shape['vocab']

    def device_step(hidden, w_head, allowed_ids, allowed_valid, target_pos):
        my_index = lax.axis_index('vocab')
        vocab_local = w_head.shape[0]
        slot_cap = 2 * allowed_ids.shape[0] // shards
        owner_id, slot_rank, local_idx = owner_layout(allowed_ids, vocab_local, shards, slot_cap, my_index)
        mine_rows = jnp.take(w_head, local_idx, axis=0)
        full_hidden = lax.all_gather(hidden, 'vocab', axis=0, tiled=True)
        own_scores = lax.dot_general(full_hidden, mine_rows, (((1,), (1,)), ((), ())), preferred_element_type=jnp.float32) * INV_TEMP
        return finish_rows(own_scores, owner_id, slot_rank, allowed_valid, target_pos, shards)

    row_spec = P(('rep', 'vocab'))
    mat_spec = P(('rep', 'vocab'), None)
    return jax.shard_map(device_step, mesh=mesh, in_specs=(mat_spec, P('vocab', None), P('rep'), P('rep'), row_spec), out_specs=(mat_spec, row_spec), check_vma=False)
```

profile of v0, /device:TPU:97, one launch (start us, length us, event | category | flops | bytes accessed | tf_op | source)
XLA Modules:
  0.0 621.0 jit_solution(18077790245291523108)
XLA Ops:
  7.3 0.7 all-gather.2.cloned.1.call-update
  8.0 14.7 %scatter_custom_fusion = s32[32]{0:T(128)S(1)} fusion(s32[2048]{0:T(1024)S(1)} %get-tuple-element.13, s32[2048]{0:T(1024)S(1)} %ne.14, s32[]{:T(128)} %constant.27.clone.1), kind=kCustom, calls=%fused_computation.47 | custom fusion | flops 2048 | bytes 132 | tf_op jit(solution)/shard_map/scatter-add | solution.py:12
  22.7 0.1 copy.10
  22.8 0.1 reduce
  23.0 0.7 fusion.16
  25.1 5.0 sort.34
  30.9 1.1 gather_fusion
  32.1 6.7 %gather_fusion.1 = bf16[128,4096]{1,0:T(8,128)(2,1)S(1)} fusion(bf16[1024,4096]{1,0:T(8,128)(2,1)} %param.6, s32[1024]{0:T(1024)S(1)} %pad_clamp_fusion), kind=kCustom, calls=%fused_computation.1 | custom fusion | bytes 2097664 | tf_op jit(solution)/shard_map/jit(_take)/gather | solution.py:42
  38.8 346.1 %all-gather.2.cloned.1.call-done = bf16[16384,4096]{1,0:T(8,128)(2,1)} async-done(((bf16[512,4096]{1,0:T(8,128)(2,1)}), bf16[16384,4096]{1,0:T(8,128)(2,1)}) %all-gather.2.cloned.1.call-update) | async-done | bytes 134217744 | tf_op jit(solution)/shard_map/all_gather | solution.py:43
  384.9 55.3 %convolution_multiply_fusion = f32[128,16384]{1,0:T(8,128)} fusion(bf16[16384,4096]{1,0:T(8,128)(2,1)} %all-gather.2.cloned.1.call-done, bf16[128,4096]{1,0:T(8,128)(2,1)S(1)} %gather_fusion.1, pred[128]{0:T(512)(128)(4,1)S(1)} %compare_and_fusion), kind=kOutput, calls=%fused_computation.5 | convolution fusion | flops 17182490624 | bytes 143655040 | tf_op jit(solution)/shard_map/dot_general | solution.py:44
  440.2 8.0 %copy.15 = f32[16,32,8,512]{3,2,0,1:T(8,128)} copy(f32[16,32,8,512]{3,2,1,0:T(8,128)} %bitcast.55) | data formatting | bytes 16777216 | tf_op jit(solution)/shard_map/reshape | solution.py:23
  448.3 4.2 all-to-all-start
  452.5 5.0 sort.35
  457.6 0.7 fusion.15
  458.3 20.1 %fusion.6 = s32[2048]{0:T(1024)S(1)} fusion(s32[2048]{0:T(1024)S(1)} %get-tuple-element.5, s32[]{:T(128)} %bitcast.5, s32[]{:T(128)} %bitcast.6, s32[]{:T(128)} %bitcast.7, s32[]{:T(128)} %bitcast.8, s32[]{:T(128)} %bitcast.9, s32[]{:T(128)} %bitcast.10, s32[]{:T(128)} %bitcast.11, s32[]{:T(128)} %bitcast.12, s32[]{:T(128)} %bitcast.13, s32[]{:T(128)} %bitcast.14, ...), kind=kLoop, calls=%fused_computation.23 | loop fusion | flops 182272 | bytes 24704 | tf_op jit(solution)/shard_map/concatenate | solution.py:25
  478.4 78.9 %all-to-all-done = f32[32,512,128]{1,2,0:T(8,128)} async-done(((f32[32,512,128]{1,2,0:T(8,128)}), f32[32,512,128]{1,2,0:T(8,128)}, u32[]{:S(2)}, u32[]{:S(2)}) %all-to-all-start) | async-done | bytes 8388640 | tf_op jit(solution)/shard_map/all_to_all | solution.py:24
  557.3 35.6 %gather_fusion.2 = f32[2048,512]{1,0:T(8,128)} fusion(f32[32,512,128]{1,2,0:T(8,128)} %all-to-all-done, s32[2048]{0:T(1024)S(1)} %fusion.6), kind=kCustom, calls=%fused_computation.2 | custom fusion | bytes 8404992 | tf_op jit(solution)/shard_map/gather | solution.py:25
  592.9 2.6 select_reduce_fusion
  595.5 0.8 copy-done
  596.3 0.9 exponential_reduce_fusion
  597.2 7.1 %gather_fusion.3 = f32[512]{0:T(512)S(1)} fusion(f32[512,2048]{0,1:T(8,128)} %bitcast.53, s32[512]{0:T(512)S(1)} %bitcast.54), kind=kCustom, calls=%fused_computation.3 | custom fusion | bytes 8192 | tf_op jit(solution)/shard_map/jit(take_along_axis)/gather | solution.py:30
  604.3 0.6 select_subtract_fusion.1
  604.9 4.0 exponential_select_fusion
  608.8 5.3 copy.12
  (25 shorter events, 0.3 us)
Async XLA Ops:
  7.2 0.8 copy-start.1
  7.2 377.7 %all-gather.2.cloned.1.call-start = ((), (), s32[]{:S(2)}) async-start(), calls=%async_computation.1 | async-start | bytes 138412032 | tf_op jit(solution)/shard_map/all_gather | solution.py:43
  448.3 9.2 %copy-start.3 = (s32[512]{0:T(512)S(1)}, s32[512]{0:T(512)}, u32[]{:S(2)}) copy-start(s32[512]{0:T(512)} %param.9) | copy-start | bytes 6148
  448.3 10.0 %copy-start.2 = (s32[2048]{0:T(1024)S(1)}, s32[2048]{0:T(1024)}, u32[]{:S(2)}) copy-start(s32[2048]{0:T(1024)} %param.8) | copy-start | bytes 24580
  448.3 109.0 %all-to-all-start = ((f32[32,512,128]{1,2,0:T(8,128)}), f32[32,512,128]{1,2,0:T(8,128)}, u32[]{:S(2)}, u32[]{:S(2)}) async-start(f32[32,512,128]{1,2,0:T(8,128)} %bitcast.56), calls=%async_computation | async-start | bytes 16777216 | tf_op jit(solution)/shard_map/all_to_all | solution.py:24
  592.9 3.4 copy-start
Sparse Core Ops, SparseCore 0:
  10.1 374.7 all-gather.1
where the time goes:
time: 630 us; the launch traced here: 621 us
  waiting for transfers between devices  426 us (68%)
  local copies, waits for them, and re-layouts  66.2 us (11%)
  matrix products  55.3 us (9%)
  other arithmetic  53.2 us (8%)
  between operations  16.3 us (3%)
    all_gather x1, waiting for transfers between devices, device_step(): full_hidden = lax.all_gather(hidden, 'vocab', axis=0, tiled=True)  346 us
    all_to_all x1, waiting for transfers between devices, finish_rows(): incoming = lax.all_to_all(outgoing, 'vocab', 0, 0)  78.9 us
    dot_general x1, matrix products, device_step(): lax.dot_general(full_hidden, mine_rows, (((1,), (1,)), ((), ())), preferr...  55.3 us
    gather x1, local copies, waits for them, and re-layouts, finish_rows(): scores = incoming[owner_id, :, slot_rank].T  35.6 us
    concatenate x1, other arithmetic, finish_rows(): scores = incoming[owner_id, :, slot_rank].T  20.1 us
    scatter-add x1, other arithmetic, owner_layout(): counts = jnp.bincount(owner_id, length=shards)  14.7 us
  transfers between devices with their start and end apart: 2, of which 2 were waited for; matrix products, arithmetic and copies ran while one was open for 9% of the time, Pallas kernels for 0%

commit v1 on v0

v1 whole, which is shorter than its diff:
```python
import jax
import jax.numpy as jnp
from jax import lax
from jax.sharding import PartitionSpec as P

INV_TEMP = 1.25


def ranks(owner, shards):
    n = owner.shape[0]
    block = 128
    hot = (owner[:, None] == jnp.arange(shards)[None, :]).astype(jnp.bfloat16).reshape(n // block, block, shards)
    below = (jnp.arange(block)[:, None] > jnp.arange(block)[None, :]).astype(jnp.bfloat16)
    inside = jnp.einsum('ij,bjs->bis', below, hot, preferred_element_type=jnp.float32)
    totals = jnp.sum(hot.astype(jnp.float32), axis=1)
    nb = n // block
    before = jnp.sum(jnp.where((jnp.arange(nb)[:, None] > jnp.arange(nb)[None, :])[:, :, None], totals[None], 0.0), axis=1)
    rank = jnp.sum((inside + before[:, None, :]) * hot.astype(jnp.float32), axis=2).reshape(n)
    return rank.astype(jnp.int32), jnp.sum(totals, axis=0).astype(jnp.int32)


def solution(mesh):
    shards = mesh.shape['vocab']

    def device_step(hidden, w_head, allowed_ids, allowed_valid, target_pos):
        me = lax.axis_index('vocab')
        vocab_local, depth = w_head.shape
        n = allowed_ids.shape[0]
        cap = 2 * n // shards
        cols = depth // shards
        owner = allowed_ids // vocab_local
        rank, counts = ranks(owner, shards)
        rounds = (jnp.max(counts) + cap - 1) // cap

        def exchange(i):
            slot = rank - i * cap
            mine = (owner == me)[None, :] & (slot[None, :] == jnp.arange(cap)[:, None])
            local = jnp.sum(jnp.where(mine, (allowed_ids - me * vocab_local)[None, :] + 1, 0), axis=1) - 1
            pick = (local[:, None] == jnp.arange(vocab_local)[None, :]).astype(jnp.bfloat16)
            rows = jnp.dot(pick, w_head, preferred_element_type=jnp.float32).astype(jnp.bfloat16)
            out = rows.reshape(cap, shards, cols).transpose(1, 0, 2)
            got = lax.all_to_all(out, 'vocab', 0, 0).reshape(shards * cap, cols)
            code = jnp.where((slot >= 0) & (slot < cap), owner * cap + slot, -1)
            place = (code[:, None] == jnp.arange(shards * cap)[None, :]).astype(jnp.bfloat16)
            return jnp.dot(place, got, preferred_element_type=jnp.float32).astype(jnp.bfloat16)

        slices = lax.fori_loop(1, rounds, lambda i, acc: acc + exchange(i), exchange(0))
        every = lax.all_gather(slices, 'vocab', axis=0)
        scores = jnp.einsum('bdk,djk->bj', hidden.reshape(hidden.shape[0], shards, cols), every, preferred_element_type=jnp.float32) * INV_TEMP
        keep = (allowed_valid > 0)[None, :]
        masked = jnp.where(keep, scores, -jnp.inf)
        log_norm = jax.nn.logsumexp(masked, axis=1)
        probs = jnp.where(keep, jnp.exp(masked - log_norm[:, None]), 0.0)
        hit = target_pos[:, None] == jnp.arange(n)[None, :]
        picked = jnp.sum(jnp.where(hit, scores, 0.0), axis=1)
        return probs, picked - log_norm

    row_spec = P(('rep', 'vocab'))
    mat_spec = P(('rep', 'vocab'), None)
    return jax.shard_map(device_step, mesh=mesh, in_specs=(mat_spec, P('vocab', None), P('rep'), P('rep'), row_spec), out_specs=(mat_spec, row_spec), check_vma=False)
```

time: 630 us -> 145 us (0.23); the launches traced: 621 us -> 145 us
  waiting for transfers between devices: 426 us -> 81.4 us
  local copies, waits for them, and re-layouts: 66.2 us -> 7.4 us
  other arithmetic: 53.2 us -> 7.1 us
  matrix products: 55.3 us -> 24.4 us
    all_gather x1, waiting for transfers between devices: 346 us -> 66.2 us  [device_step(): every = lax.all_gather(slices, 'vocab', axis=0)]
    all_to_all x1, waiting for transfers between devices: 78.9 us -> 15.2 us  [exchange(): got = lax.all_to_all(out, 'vocab', 0, 0).reshape(shards * cap, cols)]
    gather x6 -> x0, local copies, waits for them, and re-layouts: 51.9 us -> none  [the longest x1 35.6 us: finish_rows(): scores = incoming[owner_id, :, slot_rank].T]
    dot_general x1 -> x4, matrix products: 55.3 us -> 24.4 us  [the longest x1 13.6 us: device_step(): jnp.einsum('bdk,djk->bj', hidden.reshape(hidden.shape[0], shards, cols),...]
    concatenate x1 -> x0, other arithmetic: 20.1 us -> none  [finish_rows(): scores = incoming[owner_id, :, slot_rank].T]
    scatter-add x1 -> x0, other arithmetic: 14.7 us -> none  [owner_layout(): counts = jnp.bincount(owner_id, length=shards)]
    sort x2 -> x0, other arithmetic: 10.1 us -> none  [the longest x1 5.04 us: owner_layout(): sort_order = jnp.argsort(owner_id, stable=True)]
    reshape x1, local copies, waits for them, and re-layouts: 8.04 us -> 1.26 us  [exchange(): out = rows.reshape(cap, shards, cols).transpose(1, 0, 2)]
  transfers between devices with their start and end apart: 2 -> 2, of which waited for: 2 -> 2; matrix products, arithmetic and copies ran while one was open for 9% -> 0% of each run, Pallas kernels for 0% -> 0%
where the time goes in v1:
time: 145 us
  waiting for transfers between devices  81.4 us (56%)
  matrix products  24.4 us (17%)
  between operations  14.9 us (10%)
  starting transfers between devices  9.2 us (6%)
  local copies, waits for them, and re-layouts  7.4 us (5%)
  other arithmetic  7.1 us (5%)
    all_gather x1, waiting for transfers between devices, device_step(): every = lax.all_gather(slices, 'vocab', axis=0)  66.2 us
    all_to_all x1, waiting for transfers between devices, exchange(): got = lax.all_to_all(out, 'vocab', 0, 0).reshape(shards * cap, cols)  15.2 us
    dot_general x1, matrix products, device_step(): jnp.einsum('bdk,djk->bj', hidden.reshape(hidden.shape[0], shards, cols),...  13.6 us
    all_to_all x1, starting transfers between devices, exchange(): got = lax.all_to_all(out, 'vocab', 0, 0).reshape(shards * cap, cols)  9.14 us
    unnamed x9, local copies, waits for them, and re-layouts  6.14 us
    dot_general x1, matrix products, exchange(): jnp.dot(place, got, preferred_element_type=jnp.float32).astype(jnp.bfloat16)  5.86 us
    dot_general x1, matrix products, exchange(): jnp.dot(pick, w_head, preferred_element_type=jnp.float32)  4.72 us
  transfers between devices with their start and end apart: 2, of which 2 were waited for; matrix products, arithmetic and copies ran while one was open for 0% of the time, Pallas kernels for 0%

profile of v1, /device:TPU:97, one launch (start us, length us, event | category | flops | bytes accessed | tf_op | source)
XLA Modules:
  0.0 144.8 jit_solution(10298027791658911153)
XLA Ops:
  7.2 0.7 broadcast_compare_fusion.1
  7.9 0.7 subtract_add_fusion.1
  8.6 0.2 convert_reduce_fusion
  8.8 0.1 select_reduce_fusion.2
  8.9 0.2 fusion.18
  9.2 0.3 select_reduce_fusion.1
  9.5 4.7 %fusion.15 = bf16[16,32,8,128]{3,2,1,0:T(8,128)(2,1)S(1)} fusion(bf16[1024,4096]{1,0:T(8,128)(2,1)} %param.8, s32[128]{0:T(128)S(1)} %broadcast_add_fusion.1), kind=kOutput, calls=%fused_computation.34 | convolution fusion | flops 1074397184 | bytes 9437696 | tf_op jit(solution)/shard_map/dot_general | solution.py:40
  14.2 1.3 copy.29
  15.5 9.1 %all-to-all-start.1 = ((bf16[32,128,128]{2,1,0:T(8,128)(2,1)}), bf16[32,128,128]{2,1,0:T(8,128)(2,1)S(1)}, u32[]{:S(2)}, u32[]{:S(2)}) async-start(bf16[32,128,128]{2,1,0:T(8,128)(2,1)} %bitcast.69), calls=%async_computation.1 | async-start | bytes 2097152 | tf_op jit(solution)/shard_map/all_to_all | solution.py:42
  24.6 0.1 all-gather.3.cloned.1.call-start
  24.7 0.6 convert_reduce_fusion.2
  26.0 15.2 %all-to-all-done.1 = bf16[32,128,128]{2,1,0:T(8,128)(2,1)S(1)} async-done(((bf16[32,128,128]{2,1,0:T(8,128)(2,1)}), bf16[32,128,128]{2,1,0:T(8,128)(2,1)S(1)}, u32[]{:S(2)}, u32[]{:S(2)}) %all-to-all-start.1) | async-done | bytes 1048608 | tf_op jit(solution)/shard_map/all_to_all | solution.py:42
  41.2 5.9 %fusion.14 = bf16[2048,128]{1,0:T(8,128)(2,1)S(1)} fusion(bf16[4096,128]{1,0:T(8,128)(2,1)S(1)} %bitcast.85, s32[2048]{0:T(1024)S(1)} %add_select_fusion.2), kind=kOutput, calls=%fused_computation.33 | convolution fusion | flops 2156134400 | bytes 1581056 | tf_op jit(solution)/shard_map/dot_general | solution.py:45
  47.0 0.0 copy-start.2
  47.1 0.4 while.12
  47.5 0.0 copy-start
  47.5 0.8 copy-done
  48.3 0.1 all-gather.3.cloned.1.call-update
  48.4 66.2 %all-gather.3.cloned.1.call-done = bf16[65536,128]{1,0:T(8,128)(2,1)} async-done(((bf16[2048,128]{1,0:T(8,128)(2,1)}), bf16[65536,128]{1,0:T(8,128)(2,1)}) %all-gather.3.cloned.1.call-update) | async-done | bytes 16777232 | tf_op jit(solution)/shard_map/all_gather | solution.py:48
  114.6 13.6 %fusion.13 = (f32[512]{0:T(512)S(1)}, f32[2048,512,1]{1,0,2:T(8,128)S(1)}) fusion(pred[2048]{0:T(1024)(128)(4,1)S(1)} %broadcast_compare_fusion.2, bf16[32,2048,128]{2,1,0:T(8,128)(2,1)} %bitcast.86, bf16[512,4096]{1,0:T(8,128)(2,1)} %param.7), kind=kOutput, calls=%fused_computation.32 | convolution fusion | flops 8593080320 | bytes 25169920 | tf_op jit(solution)/shard_map/bdk,djk->bj/dot_general | solution.py:49
  128.2 1.4 fusion.12
  129.6 0.6 fusion.27
  130.2 2.4 %exponential_select_fusion = f32[512,2048]{0,1:T(8,128)} fusion(f32[2048,512,1]{1,0,2:T(8,128)S(1)} %get-tuple-element.149, f32[512]{0:T(512)S(1)} %get-tuple-element.144, pred[2048]{0:T(1024)(128)(4,1)S(1)} %broadcast_compare_fusion.2), kind=kLoop, calls=%fused_computation.30 | loop fusion | flops 4194304 | bytes 8392704 | tf_op jit(solution)/shard_map/jit(_where)/select_n | solution.py:53
  132.6 5.3 %copy.16 = f32[512,2048]{1,0:T(8,128)} copy(f32[512,2048]{0,1:T(8,128)} %exponential_select_fusion) | data formatting | bytes 8388608
  (11 shorter events, 0.0 us)
Async XLA Ops:
  15.5 25.7 %all-to-all-start.1 = ((bf16[32,128,128]{2,1,0:T(8,128)(2,1)}), bf16[32,128,128]{2,1,0:T(8,128)(2,1)S(1)}, u32[]{:S(2)}, u32[]{:S(2)}) async-start(bf16[32,128,128]{2,1,0:T(8,128)(2,1)} %bitcast.69), calls=%async_computation.1 | async-start | bytes 2097152 | tf_op jit(solution)/shard_map/all_to_all | solution.py:42
  24.6 90.0 %all-gather.3.cloned.1.call-start = ((), (), s32[]{:S(2)}) async-start(), calls=%async_computation.2 | async-start | bytes 17301504 | tf_op jit(solution)/shard_map/all_gather | solution.py:48
  41.2 5.9 %copy-start.1 = (s32[2048]{0:T(1024)S(1)}, s32[2048]{0:T(1024)}, u32[]{:S(2)}) copy-start(s32[2048]{0:T(1024)} %param.9) | copy-start | bytes 24580
  47.0 1.3 copy-start.2
  47.5 0.8 copy-start
  114.6 13.6 %copy-start.3 = (s32[512]{0:T(512)S(1)}, s32[512]{0:T(512)}, u32[]{:S(2)}) copy-start(s32[512]{0:T(512)} %param.11) | copy-start | bytes 6148
Sparse Core Ops, SparseCore 0:
  48.5 66.0 all-gather.2

commit v2 on v1

v2 whole, which is shorter than its diff:
```python
import functools
import math

import jax
import jax.numpy as jnp
from jax import lax
from jax.experimental import pallas as pl
from jax.experimental.pallas import tpu as pltpu
from jax.sharding import PartitionSpec as P

INV_TEMP = 1.25
F32, BF16, I32 = jnp.float32, jnp.bfloat16, jnp.int32


def ranks(owner, shards):
    n = owner.shape[0]
    block = 128
    hot = (owner[:, None] == jnp.arange(shards)[None, :]).astype(BF16).reshape(n // block, block, shards)
    below = (jnp.arange(block)[:, None] > jnp.arange(block)[None, :]).astype(BF16)
    inside = jnp.einsum('ij,bjs->bis', below, hot, preferred_element_type=F32)
    totals = jnp.sum(hot.astype(F32), axis=1)
    nb = n // block
    before = jnp.sum(jnp.where((jnp.arange(nb)[:, None] > jnp.arange(nb)[None, :])[:, :, None], totals[None], 0.0), axis=1)
    rank = jnp.sum((inside + before[:, None, :]) * hot.astype(F32), axis=2).reshape(n)
    return rank.astype(I32), jnp.sum(totals, axis=0).astype(I32)


def gather_kernel(side, cap, hid_hbm, head_hbm, pick_ref, code_ref, out_hbm,
                  hid, head, pick, made, got, part, gat, acc,
                  hid_sem, head_sem, made_sem, got_sem, ring_send, ring_recv, pair_send, pair_recv, out_sem):
    chips = side * side
    devs = 2 * chips
    cols = made.shape[2]
    listed = gat.shape[1]
    half = listed // 2
    me = lax.axis_index('vocab')
    core = lax.rem(me, 2)
    chip = me // 2
    x, y = lax.rem(chip, side), chip // side

    def dev(a, b, c):
        px = lax.rem(x + a * (1 - c) + b * c, side)
        py = lax.rem(y + a * c + b * (1 - c), side)
        return (py * side + px) * 2 + c

    barrier = pltpu.get_barrier_semaphore()

    def greet(i, _):
        pl.semaphore_signal(barrier, inc=1, device_id={'vocab': lax.rem(me + i, devs)}, device_id_type=pl.DeviceIdType.MESH)
        return 0

    def turn(i):
        return lax.rem(chip + 1 + i, chips)

    def head_copy(q):
        return pltpu.make_async_copy(head_hbm.at[:, pl.ds(pl.multiple_of(q * 2 * cols, 2 * cols), 2 * cols)], head.at[q], head_sem.at[q])

    def head_start(i, _):
        head_copy(turn(i)).start()
        return 0

    lax.fori_loop(0, chips, head_start, 0)
    lax.fori_loop(1, devs, greet, 0)
    hid_copy = pltpu.make_async_copy(hid_hbm, hid, hid_sem)
    hid_copy.start()

    lanes = lax.broadcasted_iota(I32, (cap, 128), 1)
    for c in range(pick.shape[1] // 128):
        pick[:, c * 128:(c + 1) * 128] = jnp.where(pick_ref[...] == lanes + c * 128, 1.0, 0.0).astype(BF16)

    def make(i):
        q = turn(i)
        head_copy(q).wait()
        rows = jnp.dot(pick[...], head[q], preferred_element_type=F32).astype(BF16)
        made[2 * q] = rows[:, :cols]
        made[2 * q + 1] = rows[:, cols:]

    def give(d):
        return pltpu.make_async_remote_copy(
            src_ref=made.at[d], dst_ref=got.at[me], send_sem=made_sem.at[d], recv_sem=got_sem.at[me],
            device_id={'vocab': d}, device_id_type=pl.DeviceIdType.MESH)

    def give_chip(i):
        q = turn(i)
        give(2 * q).start()
        give(2 * q + 1).start()

    make(0)
    pl.semaphore_wait(barrier, devs - 1)

    def make_step(i, _):
        make(i)
        give_chip(i - 1)
        return 0

    lax.fori_loop(1, chips, make_step, 0)
    mate = chip * 2 + 1 - core
    part[...] = jnp.zeros_like(part)
    got[me] = made[me]
    give(mate).start()

    def got_wait(r):
        pltpu.make_async_remote_copy(
            src_ref=made.at[r], dst_ref=got.at[r], send_sem=made_sem.at[r], recv_sem=got_sem.at[r],
            device_id={'vocab': r}, device_id_type=pl.DeviceIdType.MESH).wait_recv()

    step = min(2 * cap, 256)
    band = min(256, listed)

    def place(q):
        base = q * (2 * cap)
        pair = got[pl.ds(2 * q, 2)].reshape(2 * cap, cols)
        for k in range(2 * cap // step):
            slots = pair[k * step:(k + 1) * step]
            for m in range(listed // band):
                where = code_ref[pl.ds(m * band, band), :] - base - k * step
                hot = []
                for c in range(0, step, 128):
                    w = min(128, step - c)
                    ids = lax.broadcasted_iota(I32, (band, 128), 1) + c
                    hot.append(jnp.where(where == ids, 1.0, 0.0).astype(BF16)[:, :w])
                hot = jnp.concatenate(hot, axis=1) if len(hot) > 1 else hot[0]
                part[pl.ds(m * band, band), :] += jnp.dot(hot, slots, preferred_element_type=F32)

    def place_step(i, _):
        q = lax.rem(chip + chips - 1 - i, chips)
        got_wait(2 * q)
        got_wait(2 * q + 1)
        place(q)
        return 0

    lax.fori_loop(0, chips - 1, place_step, 0)
    got_wait(mate)
    place(chip)
    gat[me] = part[...].astype(BF16)
    hid_copy.wait()
    acc[...] = jnp.zeros_like(acc)

    def piece(ref, d, h):
        return ref.at[d, pl.ds(h * half, half), :]

    def slot(a, b, h):
        return ((a % side) * side + (b % side)) * 2 + h

    sent = []

    def ring(a, b, h, da, db):
        d = dev(a % side, b % side, core)
        to = dev(da % side, db % side, core)
        copy = pltpu.make_async_remote_copy(
            src_ref=piece(gat, d, h), dst_ref=piece(gat, d, h), send_sem=ring_send.at[len(sent)],
            recv_sem=ring_recv.at[slot(a - da, b - db, h)], device_id={'vocab': to}, device_id_type=pl.DeviceIdType.MESH)
        copy.start()
        sent.append(copy)

    def pair_copy(a, b, h, c):
        d = dev(a % side, b % side, c)
        return pltpu.make_async_remote_copy(
            src_ref=piece(gat, d, h), dst_ref=piece(gat, d, h), send_sem=pair_send.at[slot(a, b, h)],
            recv_sem=pair_recv.at[slot(a, b, h)], device_id={'vocab': mate}, device_id_type=pl.DeviceIdType.MESH)

    def arrive(a, b, h):
        d = dev(a % side, b % side, core)
        pltpu.make_async_remote_copy(
            src_ref=piece(gat, d, h), dst_ref=piece(gat, d, h), send_sem=ring_send.at[0],
            recv_sem=ring_recv.at[slot(a, b, h)], device_id={'vocab': mate}, device_id_type=pl.DeviceIdType.MESH).wait_recv()

    def add(a, b):
        for h in range(2):
            pair_copy(a, b, h, 1 - core).wait_recv()
        d, e = dev(a % side, b % side, core), dev(a % side, b % side, 1 - core)

        def columns(m, _):
            at = pl.ds(pl.multiple_of(m * band, band), band)
            lhs = jnp.concatenate([hid[:, pl.ds(pl.multiple_of(d * cols, cols), cols)], hid[:, pl.ds(pl.multiple_of(e * cols, cols), cols)]], axis=1)
            rhs = jnp.concatenate([gat[d, at, :], gat[e, at, :]], axis=1)
            acc[:, at] += lax.dot_general(lhs, rhs, (((1,), (1,)), ((), ())), preferred_element_type=F32)
            return 0

        lax.fori_loop(0, listed // band, columns, 0)

    far = side // 2

    def take(a, b, h):
        if (a, b) != (0, 0):
            arrive(a, b, h)
        if b == 0:
            if a == 0:
                order = (-1, 1) if h == 0 else (1, -1)
                for s in order:
                    ring(a, b, h, s, 0)
            elif a == 1 and h == 0:
                ring(a, b, h, -1, 0)
            elif a == -1 and h == 1:
                ring(a, b, h, 1, 0)
            for s in (-1, 1):
                ring(a, b, h, 0, s)
        elif b == 1 and h == 0:
            ring(a, b, h, 0, -1)
        elif b == -1 and h == 1:
            ring(a, b, h, 0, 1)
        pair_copy(a, b, h, core).start()

    for s, h in ((-1, 0), (1, 1)):
        ring(0, 0, h, s, 0)
        ring(0, 0, h, 0, s)
    for h in range(2):
        pair_copy(0, 0, h, core).start()
    for s, h in ((-1, 1), (1, 0)):
        ring(0, 0, h, s, 0)
        ring(0, 0, h, 0, s)

    schedule = [
        ('t', 1, 0, 0), ('t', -1, 0, 1), ('t', 0, 1, 0), ('t', 0, -1, 1), ('c', 0, 0),
        ('t', 1, 0, 1), ('t', -1, 0, 0), ('t', 0, 1, 1), ('t', 0, -1, 0), ('c', 1, 0),
        ('c', -1, 0), ('c', 0, 1),
        ('t', far, 0, 0), ('t', far, 0, 1), ('c', 0, -1),
        ('t', 1, 1, 0), ('t', -1, -1, 1), ('t', -1, 1, 0), ('t', 1, -1, 1), ('c', far, 0),
        ('t', 0, far, 0), ('t', 0, far, 1),
        ('t', 1, 1, 1), ('t', -1, -1, 0), ('t', -1, 1, 1), ('t', 1, -1, 0), ('c', 0, far), ('c', 1, 1), ('c', -1, -1),
        ('t', far, 1, 0), ('t', far, -1, 1), ('c', -1, 1), ('c', 1, -1),
        ('t', far, 1, 1), ('t', far, -1, 0),
        ('t', 1, far, 0), ('t', 1, far, 1), ('c', far, 1), ('t', -1, far, 0), ('t', -1, far, 1), ('c', far, -1),
        ('c', 1, far), ('c', -1, far), ('t', far, far, 0), ('t', far, far, 1), ('c', far, far),
    ]
    for what, *at in schedule:
        if what == 't':
            take(*at)
        else:
            add(*at)

    out_copy = pltpu.make_async_copy(acc, out_hbm, out_sem)
    out_copy.start()
    for copy in sent:
        copy.wait_send()
    for a in range(side):
        for b in range(side):
            for h in range(2):
                pair_copy(a, b, h, core).wait_send()

    def given(i, _):
        give(lax.rem(me + i, devs)).wait_send()
        return 0

    lax.fori_loop(1, devs, given, 0)
    out_copy.wait()


def gather_scores(shards, cap, collective_id, hidden, w_head, allowed_ids, owner, rank):
    rows, depth = hidden.shape
    n = allowed_ids.shape[0]
    vocab_local = w_head.shape[0]
    cols = depth // shards
    side = math.isqrt(shards // 2)
    me = lax.axis_index('vocab')
    mine = (owner == me)[None, :] & (rank[None, :] == jnp.arange(cap)[:, None])
    local = jnp.sum(jnp.where(mine, (allowed_ids - me * vocab_local)[None, :] + 1, 0), axis=1) - 1
    pick = jnp.broadcast_to(local[:, None], (cap, 128))
    code = jnp.broadcast_to((owner * cap + rank)[:, None], (n, 128))
    vmem = pl.BlockSpec(memory_space=pltpu.VMEM)
    hbm = pl.BlockSpec(memory_space=pl.ANY)
    dma = pltpu.SemaphoreType.DMA
    return pl.pallas_call(
        functools.partial(gather_kernel, side, cap),
        out_shape=jax.ShapeDtypeStruct((rows, n), F32),
        in_specs=[hbm, hbm, vmem, vmem],
        out_specs=hbm,
        scratch_shapes=[
            pltpu.VMEM((rows, depth), BF16),
            pltpu.VMEM((shards // 2, vocab_local, 2 * cols), BF16),
            pltpu.VMEM((cap, vocab_local), BF16),
            pltpu.VMEM((shards, cap, cols), BF16),
            pltpu.VMEM((shards, cap, cols), BF16),
            pltpu.VMEM((n, cols), F32),
            pltpu.VMEM((shards, n, cols), BF16),
            pltpu.VMEM((rows, n), F32),
            dma, dma((shards // 2,)), dma((shards,)), dma((shards,)),
            dma((30,)), dma((shards,)), dma((shards,)), dma((shards,)), dma,
        ],
        compiler_params=pltpu.CompilerParams(collective_id=collective_id, has_side_effects=True, vmem_limit_bytes=60 * 1024 * 1024),
        name=f'gather_scores_{cap}',
    )(hidden, w_head, pick, code)


def solution(mesh):
    shards = mesh.shape['vocab']

    def device_step(hidden, w_head, allowed_ids, allowed_valid, target_pos):
        vocab_local = w_head.shape[0]
        n = allowed_ids.shape[0]
        owner = allowed_ids // vocab_local
        rank, counts = ranks(owner, shards)
        caps = (2 * n // shards, vocab_local)
        run = [functools.partial(gather_scores, shards, cap, i) for i, cap in enumerate(caps)]
        scores = lax.cond(jnp.max(counts) <= caps[0], *run, hidden, w_head, allowed_ids, owner, rank) * INV_TEMP
        keep = (allowed_valid > 0)[None, :]
        masked = jnp.where(keep, scores, -jnp.inf)
        log_norm = jax.nn.logsumexp(masked, axis=1)
        probs = jnp.where(keep, jnp.exp(masked - log_norm[:, None]), 0.0)
        hit = target_pos[:, None] == jnp.arange(n)[None, :]
        picked = jnp.sum(jnp.where(hit, scores, 0.0), axis=1)
        return probs, picked - log_norm

    row_spec = P(('rep', 'vocab'))
    mat_spec = P(('rep', 'vocab'), None)
    return jax.shard_map(device_step, mesh=mesh, in_specs=(mat_spec, P('vocab', None), P('rep'), P('rep'), row_spec), out_specs=(mat_spec, row_spec), check_vma=False)
```

time: 145 us -> 106 us (0.73)
  Pallas kernels: 0 us -> 89.9 us
  waiting for transfers between devices: 81.4 us -> 0 us
  matrix products: 24.4 us -> 0.21 us
  between operations: 14.9 us -> 1.38 us
  starting transfers between devices: 9.2 us -> 0 us
  local copies, waits for them, and re-layouts: 7.4 us -> 2.62 us
  other arithmetic: 7.1 us -> 11 us
    pallas_call x0 -> x1, Pallas kernels: none -> 89.9 us  [gather_scores(): pl.pallas_call(functools.partial(gather_kernel, side, cap), out_shape=jax...]
    all_gather x1 -> x0, waiting for transfers between devices: 66.2 us -> none  [device_step(): every = lax.all_gather(slices, 'vocab', axis=0)]
    dot_general x4 -> x1, matrix products: 24.4 us -> 0.21 us  [ranks(): inside = jnp.einsum('ij,bjs->bis', below, hot, preferred_element_type=F32)]
    all_to_all x1 -> x0, waiting for transfers between devices: 15.2 us -> none  [exchange(): got = lax.all_to_all(out, 'vocab', 0, 0).reshape(shards * cap, cols)]
    all_to_all x1 -> x0, starting transfers between devices: 9.14 us -> none  [exchange(): got = lax.all_to_all(out, 'vocab', 0, 0).reshape(shards * cap, cols)]
    unnamed x9 -> x6, local copies, waits for them, and re-layouts: 6.14 us -> 0.6 us
    reduce_max x1 -> x2, other arithmetic: 0.63 us -> 3.46 us  [the longest x1 2.83 us: device_step(): log_norm = jax.nn.logsumexp(masked, axis=1)]
    broadcast_in_dim x0 -> x2, local copies, waits for them, and re-layouts: none -> 2.03 us  [the longest x1 1.3 us: gather_scores(): code = jnp.broadcast_to((owner * cap + rank)[:, None], (n, 128))]
  transfers between devices with their start and end apart: 2 -> 0, of which waited for: 2 -> 0; matrix products, arithmetic and copies ran while one was open for 0% -> 0% of each run, Pallas kernels for 0% -> 0%
where the time goes in v2:
time: 106 us; the launch traced here: 105 us
  Pallas kernels  89.9 us (85%)
  other arithmetic  11 us (10%)
  local copies, waits for them, and re-layouts  2.62 us (2%)
  between operations  1.38 us (1%)
    pallas_call x1, Pallas kernels, gather_scores(): pl.pallas_call(functools.partial(gather_kernel, side, cap), out_shape=jax...  89.9 us
    select_n x1, other arithmetic, device_step(): probs = jnp.where(keep, jnp.exp(masked - log_norm[:, None]), 0.0)  2.92 us
    reduce_max x1, other arithmetic, device_step(): log_norm = jax.nn.logsumexp(masked, axis=1)  2.83 us

profile of v2, /device:TPU:97, one launch (start us, length us, event | category | flops | bytes accessed | tf_op | source)
XLA Modules:
  0.0 105.4 jit_solution(3487247022427802232)
XLA Ops:
  0.6 0.7 add_select_fusion
  1.3 0.2 convert_reduce_fusion
  1.5 0.1 select_reduce_fusion.3
  1.7 0.2 fusion.5
  1.9 0.6 convert_reduce_fusion.2
  3.2 0.0 copy-start.1
  3.2 93.2 %conditional.1 = (f32[512,2048]{1,0:T(8,128)}) conditional(s32[]{:T(128)} %convert_element_type.24, (s32[2048]{0:T(1024)S(1)}, s32[2048]{0:T(1024)S(1)}, s32[2048]{0:T(1024)}, bf16[512,4096]{1,0:T(8,128)(2,1)}, bf16[1024,4096]{1,0:T(8,128)(2,1)}) %tuple.14, (s32[2048]{0:T(1024)S(1)}, s32[2048]{0:T(1024)S(1)}, s32[2048]{0:T(1024)}, ...), branch_computations={%region_5.7_spmd, %region_7.9_spmd} | conditional | flops 8398851 | bytes 1667120 | solution.py:295
  3.4 0.7 multiply_add_fusion.1
  4.2 0.3 select_reduce_fusion.1
  4.5 0.7 broadcast_in_dim.72.pick_ref
  5.2 1.3 %broadcast_in_dim.73.code_ref = s32[2048,128]{1,0:T(8,128)} broadcast(s32[2048]{0:T(1024)S(1)} %get-tuple-element.43), dimensions={0} | broadcast | bytes 1056768 | tf_op jit(solution)/shard_map/cond/branch_1_fun/broadcast_in_dim | solution.py:259
  6.5 89.9 %gather_scores_128.1 = f32[512,2048]{1,0:T(8,128)} custom-call(bf16[512,4096]{1,0:T(8,128)(2,1)} %get-tuple-element.28.hid_hbm, bf16[1024,4096]{1,0:T(8,128)(2,1)} %get-tuple-element.29.head_hbm, s32[128,128]{1,0:T(8,128)} %broadcast_in_dim.72.pick_ref, s32[2048,128]{1,0:T(8,128)} %broadcast_in_dim.73.code_ref), custom_call_target="tpu_custom_call" | custom-call | tf_op jit(solution)/shard_map/cond/branch_1_fun/gather_scores_128/pallas_call | solution.py:263
  96.5 0.0 copy-start.2
  96.5 0.0 copy-done.1
  96.5 0.0 copy-start
  96.5 2.8 %fusion.2 = f32[512]{0:T(512)S(1)} fusion(f32[512,2048]{1,0:T(8,128)} %get-tuple-element.47, pred[2048]{0:T(1024)(128)(4,1)S(1)} %broadcast_compare_fusion.2), kind=kLoop, calls=%fused_computation.19 | loop fusion | flops 3145216 | bytes 4198400 | tf_op jit(solution)/shard_map/reduce_max | solution.py:298
  99.3 0.0 copy-done.2
  99.3 0.6 copy-done
  99.9 2.0 %select_reduce_fusion.2 = (f32[512]{0:T(512)S(1)}, f32[512]{0:T(512)S(1)}) fusion(f32[512,2048]{1,0:T(8,128)S(1)} %copy-done, s32[512]{0:T(512)S(1)} %copy-done.2, f32[512]{0:T(512)S(1)} %is-finite_select_fusion, pred[2048]{0:T(1024)(128)(4,1)S(1)} %broadcast_compare_fusion.2), kind=kLoop, calls=%fused_computation.14 | loop fusion | flops 7339008 | bytes 4204544 | tf_op jit(solution)/shard_map/reduce_sum | solution.py:301
  101.9 0.6 fusion.13
  102.5 2.9 %exponential_select_fusion = f32[512,2048]{1,0:T(8,128)} fusion(f32[512,2048]{1,0:T(8,128)S(1)} %copy-done, f32[512]{0:T(512)S(1)} %get-tuple-element.40, pred[2048]{0:T(1024)(128)(4,1)S(1)} %broadcast_compare_fusion.2), kind=kLoop, calls=%fused_computation.16 | loop fusion | flops 4194304 | bytes 8392704 | tf_op jit(solution)/shard_map/jit(_where)/select_n | solution.py:299
  (6 shorter events, 0.0 us)
Async XLA Ops:
  3.2 93.3 %copy-start.1 = (s32[2048]{0:T(1024)S(1)}, s32[2048]{0:T(1024)}, u32[]{:S(2)}) copy-start(s32[2048]{0:T(1024)} %param.10) | copy-start | bytes 24580
  96.5 2.9 %copy-start.2 = (s32[512]{0:T(512)S(1)}, s32[512]{0:T(512)}, u32[]{:S(2)}) copy-start(s32[512]{0:T(512)} %param.11) | copy-start | bytes 6148
  96.5 3.5 %copy-start = (f32[512,2048]{1,0:T(8,128)S(1)}, f32[512,2048]{1,0:T(8,128)}, u32[]{:S(2)}) copy-start(f32[512,2048]{1,0:T(8,128)} %get-tuple-element.47) | copy-start | bytes 12582916

commit v3 on v2

v3 whole, which is shorter than its diff:
```python
import functools
import math

import jax
import jax.numpy as jnp
from jax import lax
from jax.experimental import pallas as pl
from jax.experimental.pallas import tpu as pltpu
from jax.sharding import PartitionSpec as P

INV_TEMP = 1.25
LEAD = 2
F32, BF16, I32 = jnp.float32, jnp.bfloat16, jnp.int32


def column(row):
    return jnp.transpose(jnp.broadcast_to(row, (128, 128)))


def lane_ids(rows):
    return lax.broadcasted_iota(I32, (rows, 128), 1)


def prepare(me, shards, vocab_local, cap, ids_ref, code_ref, pick):
    lanes = lane_ids(128)
    below = (lax.broadcasted_iota(I32, (128, 128), 0) > lanes).astype(F32).astype(BF16)
    before = jnp.zeros((1, 128), F32)
    mine = [jnp.zeros((1, 128), F32) for _ in range(-(-cap // 128))]
    for b in range(ids_ref.shape[0]):
        ids = column(ids_ref[b:b + 1, :].astype(F32)).astype(I32)
        owner = ids >> (vocab_local.bit_length() - 1) if vocab_local & (vocab_local - 1) == 0 else ids // vocab_local
        hot = (owner == lanes).astype(F32)
        number = jnp.dot(below, hot.astype(BF16), preferred_element_type=F32) + before
        before = before + jnp.sum(hot, axis=0, keepdims=True)
        number = jnp.sum(hot * number, axis=1, keepdims=True).astype(I32)
        code = owner * cap + number
        code_ref[b * 128:(b + 1) * 128, :] = code
        local = (ids - me * vocab_local + 1).astype(F32)
        for c in range(len(mine)):
            mine[c] += jnp.sum(jnp.where(code == lanes + (me * cap + c * 128), local, 0.0), axis=0, keepdims=True)
    for c in range(len(mine)):
        rows = min(128, cap - c * 128)
        local = (column(mine[c]) - 1.0).astype(I32)[:rows]
        for k in range(0, vocab_local, 128):
            pick[c * 128:c * 128 + rows, k:k + 128] = (local == lane_ids(rows) + k).astype(F32).astype(BF16)


def gather_kernel(side, cap, lead, group, hid_hbm, head_hbm, ids_ref, out_hbm,
                  hid, head, code_ref, pick, made, got, part, gat, acc,
                  hid_sem, head_sem, made_sem, got_sem, ring_send, ring_recv, pair_send, pair_recv, out_sem):
    chips = side * side
    devs = 2 * chips
    cols = made.shape[2]
    listed = gat.shape[1]
    half = listed // 2
    me = lax.axis_index('vocab')
    core = lax.rem(me, 2)
    chip = me // 2
    x, y = lax.rem(chip, side), chip // side

    def dev(a, b, c):
        px = lax.rem(x + a * (1 - c) + b * c, side)
        py = lax.rem(y + a * c + b * (1 - c), side)
        return (py * side + px) * 2 + c

    barrier = pltpu.get_barrier_semaphore()

    def greet(i, _):
        pl.semaphore_signal(barrier, inc=1, device_id={'vocab': lax.rem(me + i, devs)}, device_id_type=pl.DeviceIdType.MESH)
        return 0

    def turn(i):
        return lax.rem(chip + 1 + i, chips)

    def head_copy(q):
        return pltpu.make_async_copy(head_hbm.at[:, pl.ds(pl.multiple_of(q * 2 * cols, 2 * cols), 2 * cols)], head.at[q], head_sem.at[q])

    def head_start(i, _):
        head_copy(turn(i)).start()
        return 0

    lax.fori_loop(1, devs, greet, 0)
    lax.fori_loop(0, chips, head_start, 0)
    hid_copy = pltpu.make_async_copy(hid_hbm, hid, hid_sem)
    hid_copy.start()

    prepare(me, devs, head.shape[1], cap, ids_ref, code_ref, pick)

    def make(i):
        q = turn(i)
        head_copy(q).wait()
        rows = jnp.dot(pick[...], head[q], preferred_element_type=F32).astype(BF16)
        made[2 * q] = rows[:, :cols]
        made[2 * q + 1] = rows[:, cols:]

    def give(d):
        return pltpu.make_async_remote_copy(
            src_ref=made.at[d], dst_ref=got.at[me], send_sem=made_sem.at[d], recv_sem=got_sem.at[me],
            device_id={'vocab': d}, device_id_type=pl.DeviceIdType.MESH)

    def give_chip(i):
        q = turn(i)
        give(2 * q).start()
        give(2 * q + 1).start()

    def make_only(i, _):
        make(i)
        return 0

    def make_give(i, _):
        make(i)
        give_chip(i - lead)
        return 0

    def give_only(i, _):
        give_chip(i)
        return 0

    lax.fori_loop(0, lead, make_only, 0)
    pl.semaphore_wait(barrier, devs - 1)
    lax.fori_loop(lead, chips, make_give, 0)
    lax.fori_loop(chips - lead, chips - 1, give_only, 0)
    mate = chip * 2 + 1 - core
    part[...] = jnp.zeros_like(part)
    got[me] = made[me]
    give(mate).start()

    def got_wait(r):
        pltpu.make_async_remote_copy(
            src_ref=made.at[r], dst_ref=got.at[r], send_sem=made_sem.at[r], recv_sem=got_sem.at[r],
            device_id={'vocab': r}, device_id_type=pl.DeviceIdType.MESH).wait_recv()

    step = min(2 * cap, 256)
    band = min(256, listed)
    wide = listed if group > 1 else band

    def place(q):
        base = q * (2 * cap)
        pair = got[pl.ds(2 * q, 2)].reshape(2 * cap, cols)
        for k in range(2 * cap // step):
            slots = pair[k * step:(k + 1) * step]
            for m in range(listed // band):
                where = code_ref[pl.ds(m * band, band), :] - base - k * step
                hot = []
                for c in range(0, step, 128):
                    w = min(128, step - c)
                    ids = lax.broadcasted_iota(I32, (band, 128), 1) + c
                    hot.append(jnp.where(where == ids, 1.0, 0.0).astype(BF16)[:, :w])
                hot = jnp.concatenate(hot, axis=1) if len(hot) > 1 else hot[0]
                part[pl.ds(m * band, band), :] += jnp.dot(hot, slots, preferred_element_type=F32)

    def place_step(i, _):
        q = lax.rem(chip + chips - 1 - i, chips)
        got_wait(2 * q)
        got_wait(2 * q + 1)
        place(q)
        return 0

    lax.fori_loop(0, chips - 1, place_step, 0)
    got_wait(mate)
    place(chip)
    gat[me] = part[...].astype(BF16)
    hid_copy.wait()
    acc[...] = jnp.zeros_like(acc)

    def piece(ref, d, h):
        return ref.at[d, pl.ds(h * half, half), :]

    def slot(a, b, h):
        return ((a % side) * side + (b % side)) * 2 + h

    sent = []

    def ring_copy(k, a, b, h, da, db):
        d = dev(a % side, b % side, core)
        to = dev(da % side, db % side, core)
        return pltpu.make_async_remote_copy(
            src_ref=piece(gat, d, h), dst_ref=piece(gat, d, h), send_sem=ring_send.at[k],
            recv_sem=ring_recv.at[slot(a - da, b - db, h)], device_id={'vocab': to}, device_id_type=pl.DeviceIdType.MESH)

    def ring(*at):
        ring_copy(len(sent), *at).start()
        sent.append(at)

    def pair_copy(a, b, h, c):
        d = dev(a % side, b % side, c)
        return pltpu.make_async_remote_copy(
            src_ref=piece(gat, d, h), dst_ref=piece(gat, d, h), send_sem=pair_send.at[slot(a, b, h)],
            recv_sem=pair_recv.at[slot(a, b, h)], device_id={'vocab': mate}, device_id_type=pl.DeviceIdType.MESH)

    def arrive(a, b, h):
        d = dev(a % side, b % side, core)
        pltpu.make_async_remote_copy(
            src_ref=piece(gat, d, h), dst_ref=piece(gat, d, h), send_sem=ring_send.at[0],
            recv_sem=ring_recv.at[slot(a, b, h)], device_id={'vocab': mate}, device_id_type=pl.DeviceIdType.MESH).wait_recv()

    def ready(a, b):
        for h in range(2):
            pair_copy(a, b, h, 1 - core).wait_recv()

    def add(slices):
        lhs = jnp.concatenate([hid[:, pl.ds(pl.multiple_of(d * cols, cols), cols)] for d in slices], axis=1)
        for m in range(0, listed, wide):
            rhs = jnp.concatenate([gat[d, m:m + wide, :] for d in slices], axis=1)
            acc[:, m:m + wide] += lax.dot_general(lhs, rhs, (((1,), (1,)), ((), ())), preferred_element_type=F32)

    far = side // 2

    def take(a, b, h):
        if (a, b) != (0, 0):
            arrive(a, b, h)
        if b == 0:
            if a == 0:
                order = (-1, 1) if h == 0 else (1, -1)
                for s in order:
                    ring(a, b, h, s, 0)
            elif a == 1 and h == 0:
                ring(a, b, h, -1, 0)
            elif a == -1 and h == 1:
                ring(a, b, h, 1, 0)
            for s in (-1, 1):
                ring(a, b, h, 0, s)
        elif b == 1 and h == 0:
            ring(a, b, h, 0, -1)
        elif b == -1 and h == 1:
            ring(a, b, h, 0, 1)
        pair_copy(a, b, h, core).start()

    for s, h in ((-1, 0), (1, 1)):
        ring(0, 0, h, s, 0)
        ring(0, 0, h, 0, s)
    for h in range(2):
        pair_copy(0, 0, h, core).start()
    for s, h in ((-1, 1), (1, 0)):
        ring(0, 0, h, s, 0)
        ring(0, 0, h, 0, s)

    phases = [
        ([(1, 0, 0), (-1, 0, 1), (0, 1, 0), (0, -1, 1), (1, 0, 1), (-1, 0, 0), (0, 1, 1), (0, -1, 0)], [(0, 0), (1, 0)]),
        ([], [(-1, 0), (0, 1)]),
        ([(far, 0, 0), (far, 0, 1)], [(0, -1), (far, 0)]),
        ([(1, 1, 0), (-1, -1, 1), (-1, 1, 0), (1, -1, 1), (0, far, 0), (0, far, 1), (1, 1, 1), (-1, -1, 0)], [(0, far), (1, 1)]),
        ([(-1, 1, 1), (1, -1, 0), (far, 1, 0), (far, -1, 1)], [(-1, -1), (-1, 1)]),
        ([(far, 1, 1), (far, -1, 0), (1, far, 0), (1, far, 1)], [(1, -1), (far, 1)]),
        ([(-1, far, 0), (-1, far, 1)], [(far, -1), (1, far)]),
        ([(far, far, 0), (far, far, 1)], [(-1, far), (far, far)]),
    ]

    def phase(p, _):
        at = [0] * 4
        for k, (takes, adds) in enumerate(phases):
            @pl.when(p == k)
            def _():
                for t in takes:
                    take(*t)
                for t in adds:
                    ready(*t)
            for i, v in enumerate(sum(adds, ())):
                at[i] = at[i] + (p == k).astype(I32) * (v % side)
        slices = [dev(at[0], at[1], core), dev(at[0], at[1], 1 - core), dev(at[2], at[3], core), dev(at[2], at[3], 1 - core)]
        for g in range(0, 4, 2 * group):
            add(slices[g:g + 2 * group])
        return 0

    lax.fori_loop(0, len(phases), phase, 0)

    out_copy = pltpu.make_async_copy(acc, out_hbm, out_sem)
    out_copy.start()
    for k, at in enumerate(sent):
        ring_copy(k, *at).wait_send()
    for a in range(side):
        for b in range(side):
            for h in range(2):
                pair_copy(a, b, h, core).wait_send()

    def given(i, _):
        give(lax.rem(me + i, devs)).wait_send()
        return 0

    lax.fori_loop(1, devs, given, 0)
    out_copy.wait()


def gather_scores(shards, cap, group, collective_id, hidden, w_head, ids):
    rows, depth = hidden.shape
    n = ids.shape[0] * ids.shape[1]
    vocab_local = w_head.shape[0]
    cols = depth // shards
    side = math.isqrt(shards // 2)
    vmem = pl.BlockSpec(memory_space=pltpu.VMEM)
    hbm = pl.BlockSpec(memory_space=pl.ANY)
    dma = pltpu.SemaphoreType.DMA
    return pl.pallas_call(
        functools.partial(gather_kernel, side, cap, LEAD, group),
        out_shape=jax.ShapeDtypeStruct((rows, n), F32),
        in_specs=[hbm, hbm, vmem],
        out_specs=hbm,
        scratch_shapes=[
            pltpu.VMEM((rows, depth), BF16),
            pltpu.VMEM((shards // 2, vocab_local, 2 * cols), BF16),
            pltpu.VMEM((n, 128), I32),
            pltpu.VMEM((cap, vocab_local), BF16),
            pltpu.VMEM((shards, cap, cols), BF16),
            pltpu.VMEM((shards, cap, cols), BF16),
            pltpu.VMEM((n, cols), F32),
            pltpu.VMEM((shards, n, cols), BF16),
            pltpu.VMEM((rows, n), F32),
            dma, dma((shards // 2,)), dma((shards,)), dma((shards,)),
            dma((30,)), dma((shards,)), dma((shards,)), dma((shards,)), dma,
        ],
        compiler_params=pltpu.CompilerParams(collective_id=collective_id, has_side_effects=True, vmem_limit_bytes=60 * 1024 * 1024),
        name=f'gather_scores_{cap}',
    )(hidden, w_head, ids)


def finish_kernel(score_ref, valid_ref, target_ref, probs_ref, logp_ref):
    rows, n = score_ref.shape
    keep = valid_ref[...] > 0
    scores = score_ref[...] * INV_TEMP
    top = jnp.max(jnp.where(keep, scores, -jnp.inf), axis=1, keepdims=True)
    terms = jnp.where(keep, jnp.exp(scores - top), 0.0)
    total = jnp.sum(terms, axis=1, keepdims=True)
    probs_ref[...] = terms * (1.0 / total)
    target = column(target_ref[0].astype(F32)).astype(I32)[:rows]
    picked = jnp.zeros((rows, 128), F32)
    for c in range(0, n, 128):
        picked += jnp.where(target == lane_ids(rows) + c, scores[:, c:c + 128], 0.0)
    logp = jnp.sum(picked, axis=1, keepdims=True) - (top + jnp.log(total))
    logp_ref[0] = jnp.transpose(jnp.broadcast_to(logp, (rows, 128)))[:1]


def finish(scores, allowed_valid, target_pos):
    rows, n = scores.shape
    block = min(128, rows)
    probs, logp = pl.pallas_call(
        finish_kernel,
        grid=(rows // block,),
        out_shape=(jax.ShapeDtypeStruct((rows, n), F32), jax.ShapeDtypeStruct((rows // block, 1, block), F32)),
        in_specs=[pl.BlockSpec((block, n), lambda i: (i, 0)), pl.BlockSpec((1, n), lambda i: (0, 0)),
                  pl.BlockSpec((1, 1, block), lambda i: (i, 0, 0))],
        out_specs=(pl.BlockSpec((block, n), lambda i: (i, 0)), pl.BlockSpec((1, 1, block), lambda i: (i, 0, 0))),
        compiler_params=pltpu.CompilerParams(dimension_semantics=('arbitrary',)),
        name='finish',
    )(scores, allowed_valid.reshape(1, n), target_pos.reshape(rows // block, 1, block))
    return probs, logp.reshape(rows)


def solution(mesh):
    shards = mesh.shape['vocab']

    def device_step(hidden, w_head, allowed_ids, allowed_valid, target_pos):
        vocab_local = w_head.shape[0]
        n = allowed_ids.shape[0]
        counts = jnp.sum((allowed_ids // vocab_local)[None, :] == jnp.arange(shards)[:, None], axis=1)
        caps = (2 * n // shards, vocab_local)
        run = [functools.partial(gather_scores, shards, cap, 2 - i, i) for i, cap in enumerate(caps)]
        scores = lax.cond(jnp.max(counts) <= caps[0], *run, hidden, w_head, allowed_ids.reshape(n // 128, 128))
        return finish(scores, allowed_valid, target_pos)

    row_spec = P(('rep', 'vocab'))
    mat_spec = P(('rep', 'vocab'), None)
    return jax.shard_map(device_step, mesh=mesh, in_specs=(mat_spec, P('vocab', None), P('rep'), P('rep'), row_spec), out_specs=(mat_spec, row_spec), check_vma=False)
```

time: 106 us -> 86.9 us (0.82)
  other arithmetic: 11 us -> 1.49 us
  Pallas kernels: 89.9 us -> 83.6 us
  local copies, waits for them, and re-layouts: 2.62 us -> 0 us
    pallas_call x1 -> x2, Pallas kernels: 89.9 us -> 83.6 us  [the longest x1 77.9 us: gather_scores(): pl.pallas_call(functools.partial(gather_kernel, side, cap, LEAD, group),...]
    select_n x3 -> x1, other arithmetic: 3.64 us -> 0.71 us  [device_step(): allowed_ids // vocab_local]
    reduce_max x1 -> x0, other arithmetic: 2.83 us -> none  [device_step(): log_norm = jax.nn.logsumexp(masked, axis=1)]
    reduce_sum x4 -> x1, other arithmetic: 2.57 us -> 0.14 us  [device_step(): jnp.sum((allowed_ids // vocab_local)[None, :] == jnp.arange(shards)[:, No...]
    broadcast_in_dim x2 -> x0, local copies, waits for them, and re-layouts: 2.03 us -> none  [the longest x1 1.3 us: gather_scores(): code = jnp.broadcast_to((owner * cap + rank)[:, None], (n, 128))]
where the time goes in v3:
time: 86.9 us; the launch traced here: 86.6 us
  Pallas kernels  83.6 us (96%)
  other arithmetic  1.49 us (2%)
  between operations  1.29 us (1%)
    pallas_call x1, Pallas kernels, gather_scores(): pl.pallas_call(functools.partial(gather_kernel, side, cap, LEAD, group),...  77.9 us
    pallas_call x1, Pallas kernels, finish(): pl.pallas_call(finish_kernel, grid=(rows // block,), out_shape=(jax.Shape...  5.79 us

profile of v3, /device:TPU:97, one launch (start us, length us, event | category | flops | bytes accessed | tf_op | source)
XLA Modules:
  0.0 86.6 jit_solution(13655158702206701711)
XLA Ops:
  0.6 0.7 add_select_fusion
  1.3 0.1 convert_reduce_fusion
  1.5 0.6 reduce_max.9
  2.8 78.1 %conditional.1 = (f32[512,2048]{1,0:T(8,128)}) conditional(s32[]{:T(128)} %convert_element_type.7, (bf16[512,4096]{1,0:T(8,128)(2,1)}, bf16[1024,4096]{1,0:T(8,128)(2,1)}, s32[16,128]{1,0:T(8,128)}) %tuple.18, (bf16[512,4096]{1,0:T(8,128)(2,1)}, bf16[1024,4096]{1,0:T(8,128)(2,1)}, s32[16,128]{1,0:T(8,128)}) %tuple.19), branch_computations={%region_2.3_spmd, %region_3.4_spmd} | conditional | bytes 8 | solution.py:357
  3.0 77.9 %gather_scores_128.1 = f32[512,2048]{1,0:T(8,128)} custom-call(bf16[512,4096]{1,0:T(8,128)(2,1)} %get-tuple-element.18.hid_hbm, bf16[1024,4096]{1,0:T(8,128)(2,1)} %get-tuple-element.19.head_hbm, s32[16,128]{1,0:T(8,128)} %get-tuple-element.20.ids_ref), custom_call_target="tpu_custom_call" | custom-call | tf_op jit(solution)/shard_map/cond/branch_1_fun/gather_scores_128/pallas_call | solution.py:293
  80.8 5.8 %finish.1 = (f32[512,2048]{1,0:T(8,128)}, f32[4,1,128]{2,1,0:T(1,128)}) custom-call(f32[512,2048]{1,0:T(8,128)} %get-tuple-element.27.score_ref, s32[1,2048]{1,0:T(1,128)} %bitcast.6, s32[4,1,128]{2,1,0:T(1,128)} %bitcast.7), custom_call_target="tpu_custom_call" | custom-call | tf_op jit(solution)/shard_map/finish/pallas_call | solution.py:335

commit v4 on v3

--- a/solution.py
+++ b/solution.py
@@ -45,9 +45,9 @@
             pick[c * 128:c * 128 + rows, k:k + 128] = (local == lane_ids(rows) + k).astype(F32).astype(BF16)
 
 
-def gather_kernel(side, cap, lead, group, hid_hbm, head_hbm, ids_ref, out_hbm,
-                  hid, head, code_ref, pick, made, got, part, gat, acc,
-                  hid_sem, head_sem, made_sem, got_sem, ring_send, ring_recv, pair_send, pair_recv, out_sem):
+def gather_kernel(side, cap, lead, group, hid_hbm, head_hbm, ids_ref, acc,
+                  hid, head, code_ref, pick, made, got, part, gat,
+                  hid_sem, head_sem, made_sem, got_sem, ring_send, ring_recv, pair_send, pair_recv):
     chips = side * side
     devs = 2 * chips
     cols = made.shape[2]
@@ -264,8 +264,6 @@
 
     lax.fori_loop(0, len(phases), phase, 0)
 
-    out_copy = pltpu.make_async_copy(acc, out_hbm, out_sem)
-    out_copy.start()
     for k, at in enumerate(sent):
         ring_copy(k, *at).wait_send()
     for a in range(side):
@@ -278,7 +276,6 @@
         return 0
 
     lax.fori_loop(1, devs, given, 0)
-    out_copy.wait()
 
 
 def gather_scores(shards, cap, group, collective_id, hidden, w_head, ids):
@@ -290,11 +287,12 @@
     vmem = pl.BlockSpec(memory_space=pltpu.VMEM)
     hbm = pl.BlockSpec(memory_space=pl.ANY)
     dma = pltpu.SemaphoreType.DMA
+    limit = 2 * (rows * depth + vocab_local * depth + cap * (vocab_local + 2 * depth) + n * depth + 4 * n * cols) + 8 * 1024 * 1024
     return pl.pallas_call(
         functools.partial(gather_kernel, side, cap, LEAD, group),
         out_shape=jax.ShapeDtypeStruct((rows, n), F32),
         in_specs=[hbm, hbm, vmem],
-        out_specs=hbm,
+        out_specs=vmem,
         scratch_shapes=[
             pltpu.VMEM((rows, depth), BF16),
             pltpu.VMEM((shards // 2, vocab_local, 2 * cols), BF16),
@@ -304,19 +302,18 @@
             pltpu.VMEM((shards, cap, cols), BF16),
             pltpu.VMEM((n, cols), F32),
             pltpu.VMEM((shards, n, cols), BF16),
-            pltpu.VMEM((rows, n), F32),
             dma, dma((shards // 2,)), dma((shards,)), dma((shards,)),
-            dma((30,)), dma((shards,)), dma((shards,)), dma((shards,)), dma,
+            dma((30,)), dma((shards,)), dma((shards,)), dma((shards,)),
         ],
-        compiler_params=pltpu.CompilerParams(collective_id=collective_id, has_side_effects=True, vmem_limit_bytes=60 * 1024 * 1024),
+        compiler_params=pltpu.CompilerParams(collective_id=collective_id, has_side_effects=True, vmem_limit_bytes=limit),
         name=f'gather_scores_{cap}',
     )(hidden, w_head, ids)
 
 
 def finish_kernel(score_ref, valid_ref, target_ref, probs_ref, logp_ref):
-    rows, n = score_ref.shape
+    rows, n = probs_ref.shape
     keep = valid_ref[...] > 0
-    scores = score_ref[...] * INV_TEMP
+    scores = score_ref[pl.ds(pl.multiple_of(pl.program_id(0) * rows, rows), rows), :] * INV_TEMP
     top = jnp.max(jnp.where(keep, scores, -jnp.inf), axis=1, keepdims=True)
     terms = jnp.where(keep, jnp.exp(scores - top), 0.0)
     total = jnp.sum(terms, axis=1, keepdims=True)
@@ -336,10 +333,10 @@
         finish_kernel,
         grid=(rows // block,),
         out_shape=(jax.ShapeDtypeStruct((rows, n), F32), jax.ShapeDtypeStruct((rows // block, 1, block), F32)),
-        in_specs=[pl.BlockSpec((block, n), lambda i: (i, 0)), pl.BlockSpec((1, n), lambda i: (0, 0)),
+        in_specs=[pl.BlockSpec(memory_space=pltpu.VMEM), pl.BlockSpec((1, n), lambda i: (0, 0)),
                   pl.BlockSpec((1, 1, block), lambda i: (i, 0, 0))],
         out_specs=(pl.BlockSpec((block, n), lambda i: (i, 0)), pl.BlockSpec((1, 1, block), lambda i: (i, 0, 0))),
-        compiler_params=pltpu.CompilerParams(dimension_semantics=('arbitrary',)),
+        compiler_params=pltpu.CompilerParams(dimension_semantics=('arbitrary',), vmem_limit_bytes=16 * 1024 * 1024),
         name='finish',
     )(scores, allowed_valid.reshape(1, n), target_pos.reshape(rows // block, 1, block))
     return probs, logp.reshape(rows)
@@ -353,9 +350,12 @@
         n = allowed_ids.shape[0]
         counts = jnp.sum((allowed_ids // vocab_local)[None, :] == jnp.arange(shards)[:, None], axis=1)
         caps = (2 * n // shards, vocab_local)
-        run = [functools.partial(gather_scores, shards, cap, 2 - i, i) for i, cap in enumerate(caps)]
-        scores = lax.cond(jnp.max(counts) <= caps[0], *run, hidden, w_head, allowed_ids.reshape(n // 128, 128))
-        return finish(scores, allowed_valid, target_pos)
+
+        def run(i, cap):
+            return lambda hidden, w_head, ids, valid, target: finish(gather_scores(shards, cap, 2 - i, i, hidden, w_head, ids), valid, target)
+
+        runs = [run(i, cap) for i, cap in enumerate(caps)]
+        return lax.cond(jnp.max(counts) <= caps[0], *runs, hidden, w_head, allowed_ids.reshape(n // 128, 128), allowed_valid, target_pos)
 
     row_spec = P(('rep', 'vocab'))
     mat_spec = P(('rep', 'vocab'), None)

time: 86.9 us -> 83.9 us (0.965)
  Pallas kernels: 83.6 us -> 80.6 us
    pallas_call x1, Pallas kernels: 5.79 us -> 3.69 us  [finish(): pl.pallas_call(finish_kernel, grid=(rows // block,), out_shape=(jax.Shape...]
    pallas_call x1, Pallas kernels: 77.9 us -> 76.9 us  [gather_scores(): pl.pallas_call(functools.partial(gather_kernel, side, cap, LEAD, group),...]
where the time goes in v4:
time: 83.9 us; the launch traced here: 83.6 us
  Pallas kernels  80.6 us (96%)
  other arithmetic  1.49 us (2%)
  between operations  1.28 us (2%)
    pallas_call x1, Pallas kernels, gather_scores(): pl.pallas_call(functools.partial(gather_kernel, side, cap, LEAD, group),...  76.9 us
    pallas_call x1, Pallas kernels, finish(): pl.pallas_call(finish_kernel, grid=(rows // block,), out_shape=(jax.Shape...  3.69 us

profile of v4, /device:TPU:97, one launch (start us, length us, event | category | flops | bytes accessed | tf_op | source)
XLA Modules:
  0.0 83.6 jit_solution(2420369001017310952)
XLA Ops:
  0.6 0.7 add_select_fusion
  1.3 0.1 convert_reduce_fusion
  1.5 0.6 reduce_max.9
  2.8 80.9 %conditional.1 = (f32[512,2048]{1,0:T(8,128)}, f32[512]{0:T(512)}) conditional(s32[]{:T(128)} %convert_element_type.7, (bf16[512,4096]{1,0:T(8,128)(2,1)}, bf16[1024,4096]{1,0:T(8,128)(2,1)}, s32[2048]{0:T(1024)}, s32[2048]{0:T(1024)}, s32[512]{0:T(512)}) %tuple.15, (bf16[512,4096]{1,0:T(8,128)(2,1)}, bf16[1024,4096]{1,0:T(8,128)(2,1)}, ...), branch_computations={%region_2.3_spmd, %region_3.4_spmd} | conditional | bytes 16818276 | solution.py:358
  3.0 0.0 copy-start.2
  3.0 0.0 copy-start.4
  3.0 76.9 %gather_scores_128.1.score_ref = f32[512,2048]{1,0:T(8,128)S(1)} custom-call(bf16[512,4096]{1,0:T(8,128)(2,1)} %get-tuple-element.48.hid_hbm, bf16[1024,4096]{1,0:T(8,128)(2,1)} %get-tuple-element.50.head_hbm, s32[16,128]{1,0:T(8,128)} %bitcast.9), custom_call_target="tpu_custom_call" | custom-call | tf_op jit(solution)/shard_map/cond/branch_1_fun/gather_scores_128/pallas_call | solution.py:291
  79.9 0.0 copy-done.2
  79.9 0.0 copy-done.4
  80.0 3.7 %finish.3 = (f32[512,2048]{1,0:T(8,128)}, f32[4,1,128]{2,1,0:T(1,128)}) custom-call(f32[512,2048]{1,0:T(8,128)S(1)} %gather_scores_128.1.score_ref, s32[1,2048]{1,0:T(1,128)S(1)} %bitcast.11, s32[4,1,128]{2,1,0:T(1,128)S(1)} %bitcast.13), custom_call_target="tpu_custom_call" | custom-call | tf_op jit(solution)/shard_map/cond/branch_1_fun/finish/pallas_call | solution.py:332
Async XLA Ops:
  3.0 77.0 %copy-start.2 = (s32[2048]{0:T(1024)S(1)}, s32[2048]{0:T(1024)}, u32[]{:S(2)}) copy-start(s32[2048]{0:T(1024)} %get-tuple-element.52) | copy-start | bytes 24580 | tf_op jit(solution)/shard_map/cond
  3.0 77.0 %copy-start.4 = (s32[512]{0:T(512)S(1)}, s32[512]{0:T(512)}, u32[]{:S(2)}) copy-start(s32[512]{0:T(512)} %get-tuple-element.54) | copy-start | bytes 6148 | tf_op jit(solution)/shard_map/cond
